TPU v7x, 32 devices: a whole 2x2x4 slice. The times are simulated.
32 devices in a mesh: site: 2 (over y), owner: 16 (over z, x, core).
Axes of the slice: x: 2, y: 2, z: 4, core: 2. Of those that a mesh axis runs over, the one named last changes fastest.
Arguments:
- green_tensor: bfloat16 [4096, 6, 1024], P(('site', 'owner')), parts along dimension 0, may hold values from -6 to 6
- mechanism: float32 [2, 6, 2048], P(None, None, 'owner'), may hold values from -2.5 to 2.5
- point_owner: int32 [16, 128, 1], P('owner'), may hold values from 0 to 15; in each aligned block of 128 rows (0 to 127, 128 to 255, ..., all dimensions but the last counted through in order) at most 16 rows name the same one
- point_row: int32 [16, 128], P('owner'), may hold values from 0 to 127
- onset_step: int32 [16, 128], P('owner'), may hold values from 0 to 511
- slip_amount: float32 [16, 128], P('owner'), may hold values from 0.01 to 0.1
- point_count: int32 [16], P('owner'), may hold values from 12 to 128
- rake_angle: float32 [16], P('owner'), may hold values from -3.140625 to 3.140625
- slip_rate: float32 [16, 64], P('owner'), may hold values from 0.02 to 0.2
Outputs:
- seismogram: float32 [32, 1024], P(('site', 'owner')), parts along dimension 0
There are 2 independent parts, one for each index of `site`. A program takes and returns all parts, laid end to end along the dimension named above; an argument that names none is the same for every part. Nothing has to cross between parts.
Inputs may be any that keep to these rules, and one draw needn't show every extreme that they name: `point_owner`: among the 128 entries of one device's variations, at most 16 name the same owner, a bound that some block reaches of them.
All inputs are finite; a program needn't handle non-finite values.
Results may differ from a plain program's by a relative error of at most 0.0029.
Values may be sent and summed in bfloat16 or wider, within the bound.
A program may use at most 64 MiB of HBM per device.

v0:
```python
import functools

import jax
import jax.numpy as jnp
from jax import lax
from jax.experimental import pallas as pl
from jax.experimental.pallas import tpu as pltpu
from jax.sharding import PartitionSpec as P

MESH = pl.DeviceIdType.MESH
LANES = 128
GROUP = 32
TILE = 16
BATCHES = 4
SCALE = 2.0**34


def iota(shape, axis):
    return lax.broadcasted_iota(jnp.int32, shape, axis)


def kernel(
    n,
    cap,
    green_ref,
    mech_ref,
    owner_ref,
    row_ref,
    onset_ref,
    slip_ref,
    count_ref,
    rake_ref,
    rate_ref,
    out_ref,
    green,
    mech,
    traces,
    ask,
    got,
    use,
    part,
    parts,
    load_sem,
    smem_sem,
    ask_send,
    ask_recv,
    part_send,
    part_recv,
):
    me = lax.axis_index("owner")
    comps, points, length = green_ref.shape
    blocks = length // LANES
    stride = 2 * blocks + 1
    entries = row_ref.shape[1]
    taps = rate_ref.shape[1]
    groups = points // GROUP

    def peer(d):
        return lax.rem(me + 1 + d, n)

    loads = [
        pltpu.make_async_copy(
            green_ref.at[:, pl.ds(g * GROUP, GROUP)],
            green.at[:, pl.ds(g * GROUP, GROUP)],
            load_sem.at[g],
        )
        for g in range(groups)
    ]
    for load in loads:
        load.start()

    barrier = pltpu.get_barrier_semaphore()

    @pl.loop(0, n - 1)
    def _(d):
        pl.semaphore_signal(barrier, inc=1, device_id={"owner": peer(d)}, device_id_type=MESH)

    alive = iota((1, entries), 1) < count_ref[0]
    weight = jnp.where(alive, slip_ref[...], 0.0)
    rake = jnp.full((1, entries), rake_ref[0], jnp.float32)
    named = owner_ref[...] == iota((n, entries), 0)
    one_hot = named.astype(jnp.float32)
    before = (iota((entries, entries), 0) < iota((entries, entries), 1)).astype(jnp.bfloat16)
    ahead = jnp.dot(one_hot.astype(jnp.bfloat16), before, preferred_element_type=jnp.float32)
    rank = jnp.sum(one_hot * ahead, axis=0, keepdims=True)
    place = (rank == iota((LANES, entries), 0).astype(jnp.float32)).astype(jnp.float32)
    fields = jnp.concatenate(
        [
            one_hot * row_ref[...].astype(jnp.float32),
            one_hot * onset_ref[...].astype(jnp.float32),
            one_hot * (jnp.cos(rake) * weight),
            one_hot * (jnp.sin(rake) * weight),
        ],
        axis=0,
    )
    slots = lax.dot_general(
        fields,
        place,
        (((1,), (1,)), ((), ())),
        precision=lax.Precision.HIGHEST,
        preferred_element_type=jnp.float32,
    )
    rows = jnp.clip((slots[:n] + 0.5).astype(jnp.int32), 0, points - 1)
    onsets = jnp.clip((slots[n : 2 * n] + 0.5).astype(jnp.int32), 0, length - 1)
    fixed = (slots[2 * n :] * SCALE).astype(jnp.int32)
    lanes = iota((n, LANES), 1)
    table = jnp.where(lanes < cap, rows, pltpu.roll(onsets, cap, 1))
    table = jnp.where(lanes < 2 * cap, table, pltpu.roll(fixed[:n], 2 * cap, 1))
    table = jnp.where(lanes < 3 * cap, table, pltpu.roll(fixed[n:], 3 * cap, 1))
    ask[...] = table.reshape(n, 1, LANES)

    def ask_copy(d):
        to = peer(d)
        return pltpu.make_async_remote_copy(
            src_ref=ask.at[to],
            dst_ref=got.at[me],
            send_sem=ask_send.at[to],
            recv_sem=ask_recv.at[me],
            device_id={"owner": to},
            device_id_type=MESH,
        )

    pl.semaphore_wait(barrier, n - 1)

    @pl.loop(0, n - 1)
    def _(d):
        ask_copy(n - 2 - d).start()

    own_down = pltpu.make_async_copy(ask.at[me], use.at[me], smem_sem.at[me])
    own_down.start()

    traces[...] = jnp.zeros_like(traces)
    for c in range(comps):
        mech[pl.ds(2 * c, 2), :] = mech_ref[c]
    factor = mech[...].T
    for g in range(groups):
        loads[g].wait()
        for low in range(g * GROUP, (g + 1) * GROUP, TILE):
            part_of = factor[low : low + TILE]
            scale = [
                jnp.broadcast_to(part_of[:, i : i + 1], (TILE, LANES)) for i in range(2 * comps)
            ]
            for s in range(blocks):
                tiles = [
                    green[c, pl.ds(low, TILE), pl.ds(s * LANES, LANES)].astype(jnp.float32)
                    for c in range(comps)
                ]
                for k in range(2):
                    value = sum(tiles[c] * scale[2 * c + k] for c in range(comps))
                    start = (k * points + low) * stride + blocks + s
                    traces[pl.ds(start, TILE, stride=stride), :] = value.astype(
                        jnp.bfloat16
                    ).astype(jnp.float32)

    lane = iota((blocks, LANES), 1)

    def partial_sum(v):
        total = jnp.zeros((blocks, LANES), jnp.float32)
        for j in range(cap):
            row, onset, first, second = (use[v, 0, i * cap + j] for i in range(4))
            first, second = first.astype(jnp.float32), second.astype(jnp.float32)
            low = onset & (LANES - 1)
            start = row * stride + blocks - (onset >> (LANES.bit_length() - 1))
            other = start + points * stride
            same = (
                first * traces[pl.ds(start, blocks), :] + second * traces[pl.ds(other, blocks), :]
            )
            prior = (
                first * traces[pl.ds(start - 1, blocks), :]
                + second * traces[pl.ds(other - 1, blocks), :]
            )
            total += pltpu.roll(jnp.where(lane >= LANES - low, prior, same), low, 1)
        return total * (1.0 / SCALE)

    def part_copy(d):
        to = peer(d)
        return pltpu.make_async_remote_copy(
            src_ref=part.at[to],
            dst_ref=parts.at[me],
            send_sem=part_send.at[to],
            recv_sem=part_recv.at[me],
            device_id={"owner": to},
            device_id_type=MESH,
        )

    def down(source):
        return pltpu.make_async_copy(got.at[source], use.at[source], smem_sem.at[source])

    def fetch(d):
        source = peer(d)
        pltpu.make_async_copy(got.at[source], got.at[source], ask_recv.at[source]).wait()
        down(source).start()

    def serve(d):
        to = peer(d)
        down(to).wait()
        part[to] = partial_sum(to)
        part_copy(d).start()

    own_down.wait()
    own = partial_sum(me)

    edges = [(n - 1) * i // BATCHES for i in range(BATCHES + 1)]
    for i in range(BATCHES + 1):
        if i < BATCHES:
            pl.loop(edges[i], edges[i + 1])(fetch)
        if i > 0:
            pl.loop(edges[i - 1], edges[i])(serve)

    def gather(d, total):
        source = peer(d)
        pltpu.make_async_copy(parts.at[source], parts.at[source], part_recv.at[source]).wait()
        return total + parts[source]

    summed = lax.fori_loop(0, n - 1, gather, own)

    above = jnp.where(iota((blocks, LANES), 0) == 0, 0.0, pltpu.roll(summed, 1, 0))
    result = summed * rate_ref[0, 0]
    for j in range(1, taps):
        result += pltpu.roll(jnp.where(lane >= LANES - j, above, summed), j, 1) * rate_ref[0, j]
    out_ref[...] = result

    @pl.loop(0, n - 1)
    def _(d):
        ask_copy(d).wait_send()
        part_copy(d).wait_send()


def local(
    green_tensor,
    mechanism,
    point_owner,
    point_row,
    onset_step,
    slip_amount,
    point_count,
    rake_angle,
    slip_rate,
):
    n = lax.axis_size("owner")
    variations, entries = point_row.shape
    assert variations == 1
    cap = 2 * entries // n
    points, comps, length = green_tensor.shape
    blocks = length // LANES
    vmem = pl.BlockSpec(memory_space=pltpu.VMEM)
    smem = pl.BlockSpec(memory_space=pltpu.SMEM)
    out = pl.pallas_call(
        functools.partial(kernel, n, cap),
        out_shape=jax.ShapeDtypeStruct((blocks, LANES), jnp.float32),
        in_specs=[pl.BlockSpec(memory_space=pl.ANY)] + [vmem] * 5 + [smem] * 3,
        out_specs=vmem,
        scratch_shapes=[
            pltpu.VMEM((comps, points, length), jnp.bfloat16),
            pltpu.VMEM((LANES, points), jnp.float32),
            pltpu.VMEM(((2 * points + 1) * (2 * blocks + 1), LANES), jnp.float32),
            pltpu.VMEM((n, 1, LANES), jnp.int32),
            pltpu.VMEM((n, 1, LANES), jnp.int32),
            pltpu.SMEM((n, 1, LANES), jnp.int32),
            pltpu.VMEM((n, blocks, LANES), jnp.float32),
            pltpu.VMEM((n, blocks, LANES), jnp.float32),
            pltpu.SemaphoreType.DMA((points // GROUP,)),
            pltpu.SemaphoreType.DMA((n,)),
            pltpu.SemaphoreType.DMA((n,)),
            pltpu.SemaphoreType.DMA((n,)),
            pltpu.SemaphoreType.DMA((n,)),
            pltpu.SemaphoreType.DMA((n,)),
        ],
        compiler_params=pltpu.CompilerParams(collective_id=0, has_side_effects=True),
        name="seismogram",
    )(
        green_tensor.transpose(1, 0, 2),
        mechanism.transpose(1, 0, 2),
        point_owner.reshape(1, entries),
        point_row,
        onset_step,
        slip_amount,
        point_count,
        rake_angle,
        slip_rate,
    )
    return out.reshape(1, length)


def solution(mesh):
    in_specs = (
        P(("site", "owner"), None, None),
        P(None, None, "owner"),
        P("owner", None, None),
        P("owner", None),
        P("owner", None),
        P("owner", None),
        P("owner"),
        P("owner"),
        P("owner", None),
    )
    out_specs = P(("site", "owner"), None)
    return jax.shard_map(local, mesh=mesh, in_specs=in_specs, out_specs=out_specs, check_vma=False)
```

profile of v0, /device:TPU:0, one launch (start us, length us, event | category | flops | bytes accessed | tf_op | source)
XLA Modules:
  0.0 19.6 jit_solution(15172960613849871646)
XLA Ops:
  1.3 17.0 %seismogram.1 = f32[8,128]{1,0:T(8,128)} custom-call(bf16[6,128,1024]{2,1,0:T(8,128)(2,1)} %bitcast.4, f32[6,2,128]{2,1,0:T(2,128)} %bitcast.6, s32[1,128]{1,0:T(1,128)} %bitcast.7, s32[1,128]{1,0:T(1,128)} %row_ref.1, s32[1,128]{1,0:T(1,128)} %onset_ref.1, f32[1,128]{1,0:T(1,128)} %slip_ref.1, s32[1]{0:T(128)S(6)} %copy.11.count_ref, f32[1]{0:T(128)S(6)} %copy.12.rake_ref, ...), custom_call_target="tpu_custom_call" | custom-call | tf_op jit(solution)/shard_map/seismogram/pallas_call | solution.py:248
  18.3 1.3 %copy.13 = f32[1,1024]{1,0:T(1,128)} copy(f32[1,1024]{1,0:T(1,128)} %bitcast.5) | data formatting | bytes 8192
where the time goes:
time: 19.8 us; the launch traced here: 19.6 us
  Pallas kernels  17 us (86%)
  between operations  1.3 us (7%)
  local copies, waits for them, and re-layouts  1.28 us (6%)
    pallas_call x1, Pallas kernels, local(): pl.pallas_call(functools.partial(kernel, n, cap), out_shape=jax.ShapeDtyp...  17 us
    unnamed x1, local copies, waits for them, and re-layouts  1.28 us

commit v1 on v0

--- a/solution.py
+++ b/solution.py
@@ -11,8 +11,8 @@
 LANES = 128
 GROUP = 32
 TILE = 16
-BATCHES = 4
 SCALE = 2.0**34
+STORE_LIMIT = 1 << 20
 
 
 def iota(shape, axis):
@@ -22,7 +22,17 @@
 def kernel(
     n,
     cap,
-    green_ref,
+    green_hbm,
+    mech_hbm,
+    owner_hbm,
+    row_hbm,
+    onset_hbm,
+    slip_hbm,
+    count_hbm,
+    rake_hbm,
+    rate_hbm,
+    out_ref,
+    green,
     mech_ref,
     owner_ref,
     row_ref,
@@ -31,24 +41,22 @@
     count_ref,
     rake_ref,
     rate_ref,
-    out_ref,
-    green,
     mech,
     traces,
     ask,
-    got,
     use,
     part,
     parts,
     load_sem,
-    smem_sem,
+    small_sem,
+    own_sem,
     ask_send,
     ask_recv,
     part_send,
     part_recv,
 ):
     me = lax.axis_index("owner")
-    comps, points, length = green_ref.shape
+    comps, points, length = green_hbm.shape
     blocks = length // LANES
     stride = 2 * blocks + 1
     entries = row_ref.shape[1]
@@ -56,11 +64,34 @@
     groups = points // GROUP
 
     def peer(d):
-        return lax.rem(me + 1 + d, n)
-
+        return d + jnp.where(d >= me, 1, 0)
+
+    barrier = pltpu.get_barrier_semaphore()
+
+    @pl.loop(0, n - 1)
+    def _(d):
+        pl.semaphore_signal(barrier, inc=1, device_id={"owner": peer(d)}, device_id_type=MESH)
+
+    smalls = [
+        pltpu.make_async_copy(source, target, small_sem.at[i])
+        for i, (source, target) in enumerate(
+            [
+                (owner_hbm, owner_ref),
+                (row_hbm, row_ref),
+                (onset_hbm, onset_ref),
+                (slip_hbm, slip_ref),
+                (count_hbm, count_ref),
+                (rake_hbm, rake_ref),
+                (mech_hbm, mech_ref),
+                (rate_hbm, rate_ref),
+            ]
+        )
+    ]
+    for small in smalls:
+        small.start()
     loads = [
         pltpu.make_async_copy(
-            green_ref.at[:, pl.ds(g * GROUP, GROUP)],
+            green_hbm.at[:, pl.ds(g * GROUP, GROUP)],
             green.at[:, pl.ds(g * GROUP, GROUP)],
             load_sem.at[g],
         )
@@ -68,16 +99,12 @@
     ]
     for load in loads:
         load.start()
-
-    barrier = pltpu.get_barrier_semaphore()
-
-    @pl.loop(0, n - 1)
-    def _(d):
-        pl.semaphore_signal(barrier, inc=1, device_id={"owner": peer(d)}, device_id_type=MESH)
-
-    alive = iota((1, entries), 1) < count_ref[0]
+    for small in smalls:
+        small.wait()
+
+    alive = iota((1, entries), 1) < count_ref[0, 0]
     weight = jnp.where(alive, slip_ref[...], 0.0)
-    rake = jnp.full((1, entries), rake_ref[0], jnp.float32)
+    rake = jnp.full((1, entries), rake_ref[0, 0], jnp.float32)
     named = owner_ref[...] == iota((n, entries), 0)
     one_hot = named.astype(jnp.float32)
     before = (iota((entries, entries), 0) < iota((entries, entries), 1)).astype(jnp.bfloat16)
@@ -113,7 +140,7 @@
         to = peer(d)
         return pltpu.make_async_remote_copy(
             src_ref=ask.at[to],
-            dst_ref=got.at[me],
+            dst_ref=use.at[me],
             send_sem=ask_send.at[to],
             recv_sem=ask_recv.at[me],
             device_id={"owner": to},
@@ -126,7 +153,7 @@
     def _(d):
         ask_copy(n - 2 - d).start()
 
-    own_down = pltpu.make_async_copy(ask.at[me], use.at[me], smem_sem.at[me])
+    own_down = pltpu.make_async_copy(ask.at[me], use.at[me], own_sem)
     own_down.start()
 
     traces[...] = jnp.zeros_like(traces)
@@ -183,29 +210,15 @@
             device_id_type=MESH,
         )
 
-    def down(source):
-        return pltpu.make_async_copy(got.at[source], use.at[source], smem_sem.at[source])
-
-    def fetch(d):
-        source = peer(d)
-        pltpu.make_async_copy(got.at[source], got.at[source], ask_recv.at[source]).wait()
-        down(source).start()
-
-    def serve(d):
+    @pl.loop(0, n - 1)
+    def _(d):
         to = peer(d)
-        down(to).wait()
+        pltpu.make_async_copy(use.at[to], use.at[to], ask_recv.at[to]).wait()
         part[to] = partial_sum(to)
         part_copy(d).start()
 
     own_down.wait()
     own = partial_sum(me)
-
-    edges = [(n - 1) * i // BATCHES for i in range(BATCHES + 1)]
-    for i in range(BATCHES + 1):
-        if i < BATCHES:
-            pl.loop(edges[i], edges[i + 1])(fetch)
-        if i > 0:
-            pl.loop(edges[i - 1], edges[i])(serve)
 
     def gather(d, total):
         source = peer(d)
@@ -224,6 +237,12 @@
     def _(d):
         ask_copy(d).wait_send()
         part_copy(d).wait_send()
+
+
+def store(value_ref, out_ref, sem):
+    copy = pltpu.make_async_copy(value_ref, out_ref, sem)
+    copy.start()
+    copy.wait()
 
 
 def local(
@@ -243,30 +262,40 @@
     cap = 2 * entries // n
     points, comps, length = green_tensor.shape
     blocks = length // LANES
+    hbm = pl.BlockSpec(memory_space=pltpu.HBM)
     vmem = pl.BlockSpec(memory_space=pltpu.VMEM)
-    smem = pl.BlockSpec(memory_space=pltpu.SMEM)
     out = pl.pallas_call(
         functools.partial(kernel, n, cap),
-        out_shape=jax.ShapeDtypeStruct((blocks, LANES), jnp.float32),
-        in_specs=[pl.BlockSpec(memory_space=pl.ANY)] + [vmem] * 5 + [smem] * 3,
+        out_shape=pltpu.VMEM((blocks, LANES), jnp.float32),
+        in_specs=[hbm] * 9,
         out_specs=vmem,
         scratch_shapes=[
             pltpu.VMEM((comps, points, length), jnp.bfloat16),
+            pltpu.VMEM((comps, 2, points), jnp.float32),
+            pltpu.VMEM((1, entries), jnp.int32),
+            pltpu.VMEM((1, entries), jnp.int32),
+            pltpu.VMEM((1, entries), jnp.int32),
+            pltpu.VMEM((1, entries), jnp.float32),
+            pltpu.SMEM((1, 1), jnp.int32),
+            pltpu.SMEM((1, 1), jnp.float32),
+            pltpu.SMEM(slip_rate.shape, jnp.float32),
             pltpu.VMEM((LANES, points), jnp.float32),
             pltpu.VMEM(((2 * points + 1) * (2 * blocks + 1), LANES), jnp.float32),
-            pltpu.VMEM((n, 1, LANES), jnp.int32),
             pltpu.VMEM((n, 1, LANES), jnp.int32),
             pltpu.SMEM((n, 1, LANES), jnp.int32),
             pltpu.VMEM((n, blocks, LANES), jnp.float32),
             pltpu.VMEM((n, blocks, LANES), jnp.float32),
             pltpu.SemaphoreType.DMA((points // GROUP,)),
-            pltpu.SemaphoreType.DMA((n,)),
+            pltpu.SemaphoreType.DMA((8,)),
+            pltpu.SemaphoreType.DMA,
             pltpu.SemaphoreType.DMA((n,)),
             pltpu.SemaphoreType.DMA((n,)),
             pltpu.SemaphoreType.DMA((n,)),
             pltpu.SemaphoreType.DMA((n,)),
         ],
-        compiler_params=pltpu.CompilerParams(collective_id=0, has_side_effects=True),
+        compiler_params=pltpu.CompilerParams(
+            collective_id=0, has_side_effects=True
+        ),
         name="seismogram",
     )(
         green_tensor.transpose(1, 0, 2),
@@ -275,11 +304,20 @@
         point_row,
         onset_step,
         slip_amount,
-        point_count,
-        rake_angle,
+        point_count.reshape(1, 1),
+        rake_angle.reshape(1, 1),
         slip_rate,
     )
-    return out.reshape(1, length)
+    result = pl.pallas_call(
+        store,
+        out_shape=jax.ShapeDtypeStruct((blocks, LANES), jnp.float32),
+        in_specs=[vmem],
+        out_specs=pl.BlockSpec(memory_space=pl.ANY),
+        scratch_shapes=[pltpu.SemaphoreType.DMA],
+        compiler_params=pltpu.CompilerParams(vmem_limit_bytes=STORE_LIMIT),
+        name="store",
+    )(out)
+    return result.reshape(1, length)
 
 
 def solution(mesh):

time: 19.8 us -> 17.4 us (0.88)
  local copies, waits for them, and re-layouts: 1.28 us -> 0 us
  Pallas kernels: 17 us -> 15.9 us
    unnamed x1 -> x0, local copies, waits for them, and re-layouts: 1.28 us -> none
    pallas_call x1 -> x2, Pallas kernels: 17 us -> 15.9 us  [the longest x1 15.3 us: local(): pl.pallas_call(functools.partial(kernel, n, cap), out_shape=pltpu.VMEM((b...]
where the time goes in v1:
time: 17.4 us; the launch traced here: 17.3 us
  Pallas kernels  15.9 us (91%)
  between operations  1.3 us (7%)
    pallas_call x1, Pallas kernels, local(): pl.pallas_call(functools.partial(kernel, n, cap), out_shape=pltpu.VMEM((b...  15.3 us
    pallas_call x1, Pallas kernels, local(): pl.pallas_call(store, out_shape=jax.ShapeDtypeStruct((blocks, LANES), jnp...  0.6 us

profile of v1, /device:TPU:0, one launch (start us, length us, event | category | flops | bytes accessed | tf_op | source)
XLA Modules:
  0.0 17.3 jit_solution(12640117153420914755)
XLA Ops:
  1.3 15.3 %seismogram.1.value_ref = f32[8,128]{1,0:T(8,128)S(1)} custom-call(bf16[6,128,1024]{2,1,0:T(8,128)(2,1)} %bitcast.8, f32[6,2,128]{2,1,0:T(2,128)} %bitcast.9, s32[1,128]{1,0:T(1,128)} %bitcast.10, s32[1,128]{1,0:T(1,128)} %row_hbm.1, s32[1,128]{1,0:T(1,128)} %onset_hbm.1, f32[1,128]{1,0:T(1,128)} %slip_hbm.1, s32[1,1]{1,0:T(1,128)} %bitcast.6.count_hbm, ...), custom_call_target="tpu_custom_call" | custom-call | tf_op jit(solution)/shard_map/seismogram/pallas_call | solution.py:267
  16.6 0.6 %store.1 = f32[8,128]{1,0:T(8,128)} custom-call(f32[8,128]{1,0:T(8,128)S(1)} %seismogram.1.value_ref), custom_call_target="tpu_custom_call" | custom-call | tf_op jit(solution)/shard_map/store/pallas_call | solution.py:311
